TPU v7x, 32 devices: a whole 2x2x4 slice. The times are simulated.
32 devices in a mesh: owner: 4 (over y, core), rows: 8 (over z, x).
Axes of the slice: x: 2, y: 2, z: 4, core: 2. Of those that a mesh axis runs over, the one named last changes fastest.
Arguments:
- train_gate: float32 [64, 2048, 1024], P('owner', 'rows'), may hold values from -0.1875 to 0.1875
- other_gate: bfloat16 [64, 2048, 1024], P('owner', 'rows'), may hold values from -0.0625 to 0.0625
- train_up: float32 [64, 2048, 1024], P('owner', 'rows'), may hold values from -0.1875 to 0.1875
- other_up: bfloat16 [64, 2048, 1024], P('owner', 'rows'), may hold values from -0.0625 to 0.0625
- train_down: float32 [64, 1024, 2048], P('owner', None, 'rows'), may hold values from -0.25 to 0.25
- other_down: bfloat16 [64, 1024, 2048], P('owner', None, 'rows'), may hold values from -0.09375 to 0.09375
- router_weight: float32 [2048, 64], P('rows', 'owner'), may hold values from -0.125 to 0.125
- router_gain: float32 [2048], P('rows'), may hold values from 0.25 to 1.75
Outputs:
- ready_gate: bfloat16 [64, 2048, 1024], P('owner', None, 'rows')
- ready_up: bfloat16 [64, 2048, 1024], P('owner', None, 'rows')
- ready_down: bfloat16 [64, 1024, 2048], P('owner', 'rows')
- scale_gate: float32 [64, 1024], P('owner', 'rows')
- scale_up: float32 [64, 1024], P('owner', 'rows')
- scale_down: float32 [64, 1024], P('owner', 'rows')
- serve_router: bfloat16 [2048, 64], replicated
All inputs are finite; a program needn't handle non-finite values. Where the computation divides by a largest or mean magnitude, that divisor is 1e-20 or more.
Results may differ from a plain program's by a relative error of at most 0.001.
Values may be sent and summed in bfloat16 or wider, within the bound.
A program may use at most 192 MiB of HBM per device.

v0:
```python
import jax
import jax.numpy as jnp
from jax import lax
from jax.sharding import PartitionSpec as P


def shards(
    train_gate, other_gate, train_up, other_up, train_down, other_down, router_weight, router_gain
):
    latest_gate = train_gate + other_gate.astype(jnp.float32)
    latest_up = train_up + other_up.astype(jnp.float32)
    latest_down = train_down + other_down.astype(jnp.float32)
    scale_gate, scale_up, scale_down = lax.pmax(
        (
            jnp.max(jnp.abs(latest_gate), axis=1),
            jnp.max(jnp.abs(latest_up), axis=1),
            jnp.max(jnp.abs(latest_down), axis=2),
        ),
        "rows",
    )
    narrow_gate, narrow_up, narrow_down = (
        (latest_gate / jnp.expand_dims(scale_gate, 1)).astype(jnp.bfloat16),
        (latest_up / jnp.expand_dims(scale_up, 1)).astype(jnp.bfloat16),
        (latest_down / jnp.expand_dims(scale_down, 2)).astype(jnp.bfloat16),
    )
    ready_gate, ready_up = (
        lax.all_to_all(narrow_gate, "rows", split_axis=2, concat_axis=1, tiled=True),
        lax.all_to_all(narrow_up, "rows", split_axis=2, concat_axis=1, tiled=True),
    )
    ready_down = lax.all_to_all(narrow_down, "rows", split_axis=1, concat_axis=2, tiled=True)
    scale_gate = lax.dynamic_slice_in_dim(
        scale_gate, lax.axis_index("rows") * ready_gate.shape[2], ready_gate.shape[2], axis=1
    )
    scale_up = lax.dynamic_slice_in_dim(
        scale_up, lax.axis_index("rows") * ready_up.shape[2], ready_up.shape[2], axis=1
    )
    scale_down = lax.dynamic_slice_in_dim(
        scale_down, lax.axis_index("rows") * ready_down.shape[1], ready_down.shape[1], axis=1
    )
    part_router = (router_weight * router_gain[:, None]).astype(jnp.bfloat16)
    row_router = lax.all_gather(part_router, "rows", axis=0, tiled=True)
    serve_router = lax.all_gather(row_router, "owner", axis=1, tiled=True)
    return (ready_gate, ready_up, ready_down, scale_gate, scale_up, scale_down, serve_router)


def solution(mesh):
    placed = (
        P("owner", "rows", None),
        P("owner", "rows", None),
        P("owner", "rows", None),
        P("owner", "rows", None),
        P("owner", None, "rows"),
        P("owner", None, "rows"),
        P("rows", "owner"),
        P("rows"),
    )
    return jax.shard_map(
        shards,
        mesh=mesh,
        in_specs=placed,
        out_specs=(
            P("owner", None, "rows"),
            P("owner", None, "rows"),
            P("owner", "rows", None),
            P("owner", "rows"),
            P("owner", "rows"),
            P("owner", "rows"),
            P(),
        ),
        check_vma=False,
    )
```

profile of v0, /device:TPU:0, one launch (start us, length us, event | category | flops | bytes accessed | tf_op | source)
XLA Modules:
  0.0 877.2 jit_solution(6322543164802641597)
XLA Ops:
  7.2 0.0 all-reduce.3.cloned.1.call-start
  7.2 17.6 %copy.34 = f32[16,256,1024]{1,0,2:T(8,128)} copy(f32[16,256,1024]{2,1,0:T(8,128)} %param.10) | data formatting | bytes 33554432 | tf_op args[2]
  24.8 12.5 %copy.33 = bf16[16,256,1024]{1,0,2:T(8,128)(2,1)} copy(bf16[16,256,1024]{2,1,0:T(8,128)(2,1)} %param.11) | data formatting | bytes 16777216 | tf_op args[3]
  37.3 17.6 %copy.31 = f32[16,256,1024]{1,0,2:T(8,128)} copy(f32[16,256,1024]{2,1,0:T(8,128)} %param.8) | data formatting | bytes 33554432 | tf_op args[0]
  54.9 12.5 %copy.30 = bf16[16,256,1024]{1,0,2:T(8,128)(2,1)} copy(bf16[16,256,1024]{2,1,0:T(8,128)(2,1)} %param.9) | data formatting | bytes 16777216 | tf_op args[1]
  67.4 11.1 %abs_reduce_fusion.1 = f32[16,1024]{0,1:T(8,128)} fusion(f32[16,256,1024]{1,0,2:T(8,128)} %copy.34, bf16[16,256,1024]{1,0,2:T(8,128)(2,1)} %copy.33), kind=kLoop, calls=%fused_computation.4 | loop fusion | flops 16760832 | bytes 25231360 | tf_op jit(solution)/shard_map/reduce_max | solution.py:16
  78.5 2.1 copy-done
  80.6 2.4 copy-done.1
  83.0 4.3 abs_reduce_fusion.2
  87.3 0.0 slice-done
  87.3 29.3 %abs_reduce_fusion = f32[16,1024]{0,1:T(8,128)} fusion(f32[16,1024,256]{2,1,0:T(8,128)} %param.12, bf16[16,1024,256]{2,1,0:T(8,128)(2,1)S(1)} %bitcast.14), kind=kLoop, calls=%fused_computation.2 | loop fusion | flops 16760832 | bytes 25231360 | tf_op jit(solution)/shard_map/reduce_max | solution.py:17
  116.5 0.0 all-reduce.3.cloned.1.call-update
  116.6 92.5 %all-reduce.3.cloned.1.call-done = (f32[16,1024]{0,1:T(8,128)}, f32[16,1024]{0,1:T(8,128)}, f32[16,1024]{0,1:T(8,128)}) async-done(((f32[16,1024]{0,1:T(8,128)}, f32[16,1024]{0,1:T(8,128)}, f32[16,1024]{0,1:T(8,128)}), (f32[16,1024]{0,1:T(8,128)}, f32[16,1024]{0,1:T(8,128)}, f32[16,1024]{0,1:T(8,128)})) %all-reduce.3.cloned.1.call-update) | async-done | bytes 196624 | tf_op jit(solution)/shard_map/pmax | solution.py:13
  209.0 20.5 %divide_convert_fusion.1 = (bf16[16,256,1024]{1,0,2:T(8,128)(2,1)}, bf16[16,256,1024]{1,0,2:T(8,128)(2,1)S(1)}) fusion(f32[16,256,1024]{1,0,2:T(8,128)} %copy.34, bf16[16,256,1024]{1,0,2:T(8,128)(2,1)} %copy.33, f32[16,1024]{0,1:T(8,128)} %get-tuple-element.15, f32[16,1024]{0,1:T(8,128)} %get-tuple-element.14, f32[16,256,1024]{1,0,2:T(8,128)} %copy.31, ...), kind=kLoop, calls=%fused_computation.3 | loop fusion | flops 33554432 | bytes 67239936 | tf_op jit(solution)/shard_map/convert_element_type | solution.py:23
  229.6 187.0 %all_to_all.54 = bf16[16,256,1024]{1,0,2:T(8,128)(2,1)} all-to-all(bf16[16,256,1024]{1,0,2:T(8,128)(2,1)S(1)} %get-tuple-element.18), channel_id=1, replica_groups=mesh['owner'=4,'rows'=8] {'rows'}, dimensions={2} | all-to-all | bytes 16777216 | tf_op jit(solution)/shard_map/all_to_all | solution.py:27
  416.6 4.9 all-to-all-start.1
  421.5 23.8 %divide_convert_fusion = bf16[16,1024,256]{2,0,1:T(8,128)(2,1)} fusion(f32[16,1024,256]{2,1,0:T(8,128)} %param.12, f32[16,1024]{0,1:T(8,128)S(1)} %copy-done.2, bf16[16,1024,256]{2,1,0:T(8,128)(2,1)} %param.13), kind=kLoop, calls=%fused_computation.1 | loop fusion | flops 16777216 | bytes 33619968 | tf_op jit(solution)/shard_map/convert_element_type | solution.py:24
  445.3 158.3 %all-to-all-done.1 = bf16[16,256,1024]{1,0,2:T(8,128)(2,1)} async-done(((bf16[16,256,1024]{1,0,2:T(8,128)(2,1)}), bf16[16,256,1024]{1,0,2:T(8,128)(2,1)}, u32[]{:S(2)}, u32[]{:S(2)}) %all-to-all-start.1) | async-done | bytes 8388640 | tf_op jit(solution)/shard_map/all_to_all | solution.py:28
  603.6 5.0 all-to-all-start.2
  608.7 201.9 %all_gather.6 = bf16[2048,16]{0,1:T(8,128)(2,1)S(1)} all-gather(bf16[256,16]{0,1:T(8,128)(2,1)S(1)} %multiply_convert_fusion), channel_id=1, replica_groups=mesh['owner'=4,'rows'=8] {'rows'}, dimensions={0}, use_global_device_ids=true | all-gather | bytes 73728 | tf_op jit(solution)/shard_map/all_gather | solution.py:41
  810.6 6.0 all_gather.7
  816.5 0.8 constant_dynamic-slice_fusion
  817.4 0.7 copy.40
  818.1 0.7 copy.41
  818.7 0.8 constant_dynamic-slice_fusion.2
  819.6 0.7 copy.39
  820.2 12.3 %copy.32 = bf16[16,8,256,128]{3,2,1,0:T(8,128)(2,1)} copy(bf16[16,8,256,128]{2,0,3,1:T(8,128)(2,1)} %bitcast.15) | data formatting | bytes 16777216 | tf_op jit(solution)/shard_map/all_to_all | solution.py:27
  832.5 12.3 %copy.35 = bf16[16,8,256,128]{3,2,1,0:T(8,128)(2,1)} copy(bf16[16,8,256,128]{2,0,3,1:T(8,128)(2,1)} %bitcast.4) | data formatting | bytes 16777216 | tf_op jit(solution)/shard_map/all_to_all | solution.py:28
  844.8 0.0 all-to-all-done.2
  844.8 11.4 %copy.38 = bf16[16,128,8,256]{3,2,1,0:T(8,128)(2,1)} copy(bf16[16,128,8,256]{3,0,1,2:T(8,128)(2,1)} %bitcast.7) | data formatting | bytes 16777216 | tf_op jit(solution)/shard_map/all_to_all | solution.py:30
  856.2 13.4 %all_to_all.50 = bf16[16,128,2048]{2,1,0:T(8,128)(2,1)} reshape(bf16[16,128,8,256]{3,2,1,0:T(8,128)(2,1)} %copy.38) | data formatting | bytes 16777216 | tf_op jit(solution)/shard_map/all_to_all | solution.py:30
  869.6 0.7 copy.53
  (13 shorter events, 0.0 us)
Async XLA Ops:
  7.2 201.9 %all-reduce.3.cloned.1.call-start = ((), (), s32[]{:S(2)}) async-start(), calls=%async_computation.3 | async-start | bytes 3145728 | tf_op jit(solution)/shard_map/pmax | solution.py:13
  67.4 13.2 %copy-start = (f32[16,256,1024]{1,0,2:T(8,128)S(1)}, f32[16,256,1024]{1,0,2:T(8,128)}, u32[]{:S(2)}) copy-start(f32[16,256,1024]{1,0,2:T(8,128)} %copy.31) | copy-start | bytes 50331652
  67.4 15.6 %copy-start.1 = (bf16[16,256,1024]{1,0,2:T(8,128)(2,1)S(1)}, bf16[16,256,1024]{1,0,2:T(8,128)(2,1)}, u32[]{:S(2)}) copy-start(bf16[16,256,1024]{1,0,2:T(8,128)(2,1)} %copy.30) | copy-start | bytes 25165828
  67.4 19.9 %slice-start = ((s8[8388608]{0:T(1024)(128)(4,1)}), s8[4194304]{0:T(1024)(128)(4,1)S(1)}, s32[]{:S(2)}) async-start(s8[8388608]{0:T(1024)(128)(4,1)} %bitcast.13), calls=%async_computation.4 | async-start | bytes 8388608
  83.0 4.3 slice-start.1
  229.6 192.0 %copy-start.2 = (f32[16,1024]{0,1:T(8,128)S(1)}, f32[16,1024]{0,1:T(8,128)}, u32[]{:S(2)}) copy-start(f32[16,1024]{0,1:T(8,128)} %get-tuple-element.16) | copy-start | bytes 196612
  416.6 187.0 %all-to-all-start.1 = ((bf16[16,256,1024]{1,0,2:T(8,128)(2,1)}), bf16[16,256,1024]{1,0,2:T(8,128)(2,1)}, u32[]{:S(2)}, u32[]{:S(2)}) async-start(bf16[16,256,1024]{1,0,2:T(8,128)(2,1)} %get-tuple-element.17), calls=%async_computation.1 | async-start | bytes 16777216 | tf_op jit(solution)/shard_map/all_to_all | solution.py:28
  445.3 163.3 %copy-start.3 = (f32[256,16]{0,1:T(8,128)S(1)}, f32[256,16]{0,1:T(8,128)}, u32[]{:S(2)}) copy-start(f32[256,16]{0,1:T(8,128)} %param.14) | copy-start | bytes 49156
  445.3 163.3 %copy-start.4 = (f32[256]{0:T(256)S(1)}, f32[256]{0:T(256)}, u32[]{:S(2)}) copy-start(f32[256]{0:T(256)} %param.15) | copy-start | bytes 3076
  603.6 241.2 %all-to-all-start.2 = ((bf16[16,1024,256]{2,0,1:T(8,128)(2,1)}), bf16[16,1024,256]{2,0,1:T(8,128)(2,1)}, u32[]{:S(2)}, u32[]{:S(2)}) async-start(bf16[16,1024,256]{2,0,1:T(8,128)(2,1)} %divide_convert_fusion), calls=%async_computation.2 | async-start | bytes 16777216 | tf_op jit(solution)/shard_map/all_to_all | solution.py:30
Sparse Core Ops, SparseCore 0:
  116.7 92.2 all-reduce.2
where the time goes:
time: 880 us; the launch traced here: 877 us
  blocking collectives  395 us (45%)
  waiting for transfers between devices  251 us (29%)
  local copies, waits for them, and re-layouts  118 us (13%)
  other arithmetic  88.9 us (10%)
  between operations  14.1 us (2%)
  starting transfers between devices  10 us (1%)
    all_gather x1, blocking collectives, shards(): row_router = lax.all_gather(part_router, 'rows', axis=0, tiled=True)  202 us
    all_to_all x1, blocking collectives, shards(): lax.all_to_all(narrow_gate, 'rows', split_axis=2, concat_axis=1, tiled=True)  187 us
    all_to_all x1, waiting for transfers between devices, shards(): lax.all_to_all(narrow_up, 'rows', split_axis=2, concat_axis=1, tiled=True)  158 us
    pmax x1, waiting for transfers between devices, shards(): lax.pmax((jnp.max(jnp.abs(latest_gate), axis=1), jnp.max(jnp.abs(latest_u...  92.5 us
    unnamed x22, local copies, waits for them, and re-layouts  67.4 us
    reduce_max x1, other arithmetic, shards(): jnp.max(jnp.abs(latest_down), axis=2)  29.3 us
    all_to_all x2, local copies, waits for them, and re-layouts, shards(): lax.all_to_all(narrow_down, 'rows', split_axis=1, concat_axis=2, tiled=True)  24.8 us
    convert_element_type x1, other arithmetic, shards(): (latest_down / jnp.expand_dims(scale_down, 2)).astype(jnp.bfloat16)  23.8 us
  transfers between devices with their start and end apart: 3, of which 2 were waited for; matrix products, arithmetic and copies ran while one was open for 6% of the time, Pallas kernels for 0%

commit v1 on v0

--- a/solution.py
+++ b/solution.py
@@ -2,6 +2,13 @@
 import jax.numpy as jnp
 from jax import lax
 from jax.sharding import PartitionSpec as P
+
+
+def _process_node(z, axis_name):
+    shaped = jnp.stack([z for _ in range(lax.axis_size(axis_name))])
+    row_out = lax.all_to_all(shaped, axis_name, 0, 0)
+    kept_arr = jnp.concatenate(row_out, 0)
+    return kept_arr
 
 
 def shards(
@@ -38,7 +45,7 @@
         scale_down, lax.axis_index("rows") * ready_down.shape[1], ready_down.shape[1], axis=1
     )
     part_router = (router_weight * router_gain[:, None]).astype(jnp.bfloat16)
-    row_router = lax.all_gather(part_router, "rows", axis=0, tiled=True)
+    row_router = _process_node(part_router, "rows")
     serve_router = lax.all_gather(row_router, "owner", axis=1, tiled=True)
     return (ready_gate, ready_up, ready_down, scale_gate, scale_up, scale_down, serve_router)
 

time: 880 us -> 832 us (0.945)
  blocking collectives: 395 us -> 195 us
  waiting for transfers between devices: 251 us -> 392 us
    all_gather x1 -> x0, blocking collectives: 202 us -> none  [shards(): row_router = lax.all_gather(part_router, 'rows', axis=0, tiled=True)]
    all_to_all x1, waiting for transfers between devices: 0.01 us -> 148 us  [shards(): lax.all_to_all(narrow_down, 'rows', split_axis=1, concat_axis=2, tiled=True)]
  transfers between devices with their start and end apart: 3 -> 4, of which waited for: 2 -> 3; matrix products, arithmetic and copies ran while one was open for 6% -> 9% of each run, Pallas kernels for 0% -> 0%
where the time goes in v1:
time: 832 us; the launch traced here: 830 us
  waiting for transfers between devices  392 us (47%)
  blocking collectives  195 us (23%)
  local copies, waits for them, and re-layouts  119 us (14%)
  other arithmetic  91.9 us (11%)
  starting transfers between devices  17.3 us (2%)
  between operations  14.1 us (2%)
    all_to_all x1, blocking collectives, shards(): lax.all_to_all(narrow_gate, 'rows', split_axis=2, concat_axis=1, tiled=True)  189 us
    all_to_all x1, waiting for transfers between devices, shards(): lax.all_to_all(narrow_up, 'rows', split_axis=2, concat_axis=1, tiled=True)  159 us
    all_to_all x1, waiting for transfers between devices, shards(): lax.all_to_all(narrow_down, 'rows', split_axis=1, concat_axis=2, tiled=True)  148 us
    pmax x1, waiting for transfers between devices, shards(): lax.pmax((jnp.max(jnp.abs(latest_gate), axis=1), jnp.max(jnp.abs(latest_u...  85.9 us
    unnamed x22, local copies, waits for them, and re-layouts  67.4 us
    reduce_max x1, other arithmetic, shards(): jnp.max(jnp.abs(latest_down), axis=2)  29.3 us
    all_to_all x2, local copies, waits for them, and re-layouts, shards(): lax.all_to_all(narrow_down, 'rows', split_axis=1, concat_axis=2, tiled=True)  24.8 us
    convert_element_type x1, other arithmetic, shards(): (latest_down / jnp.expand_dims(scale_down, 2)).astype(jnp.bfloat16)  23.8 us
  transfers between devices with their start and end apart: 4, of which 3 were waited for; matrix products, arithmetic and copies ran while one was open for 9% of the time, Pallas kernels for 0%

profile of v1, /device:TPU:0, one launch (start us, length us, event | category | flops | bytes accessed | tf_op | source)
XLA Modules:
  0.0 829.8 jit_solution(11450437637752484735)
XLA Ops:
  7.2 0.0 all-reduce.3.cloned.1.call-start
  7.2 17.6 %copy.47 = f32[16,256,1024]{1,0,2:T(8,128)} copy(f32[16,256,1024]{2,1,0:T(8,128)} %param.10) | data formatting | bytes 33554432 | tf_op args[2]
  24.8 12.5 %copy.46 = bf16[16,256,1024]{1,0,2:T(8,128)(2,1)} copy(bf16[16,256,1024]{2,1,0:T(8,128)(2,1)} %param.11) | data formatting | bytes 16777216 | tf_op args[3]
  37.3 17.6 %copy.44 = f32[16,256,1024]{1,0,2:T(8,128)} copy(f32[16,256,1024]{2,1,0:T(8,128)} %param.8) | data formatting | bytes 33554432 | tf_op args[0]
  54.9 12.5 %copy.43 = bf16[16,256,1024]{1,0,2:T(8,128)(2,1)} copy(bf16[16,256,1024]{2,1,0:T(8,128)(2,1)} %param.9) | data formatting | bytes 16777216 | tf_op args[1]
  67.4 11.1 %abs_reduce_fusion.1 = f32[16,1024]{0,1:T(8,128)} fusion(f32[16,256,1024]{1,0,2:T(8,128)} %copy.47, bf16[16,256,1024]{1,0,2:T(8,128)(2,1)} %copy.46), kind=kLoop, calls=%fused_computation.4 | loop fusion | flops 16760832 | bytes 25231360 | tf_op jit(solution)/shard_map/reduce_max | solution.py:23
  78.5 2.1 copy-done
  80.6 2.4 copy-done.1
  83.0 4.3 abs_reduce_fusion.2
  87.2 29.3 %abs_reduce_fusion = f32[16,1024]{0,1:T(8,128)} fusion(f32[16,1024,256]{2,1,0:T(8,128)} %param.12, bf16[16,1024,256]{2,1,0:T(8,128)(2,1)S(1)} %bitcast.16), kind=kLoop, calls=%fused_computation.2 | loop fusion | flops 16760832 | bytes 25231360 | tf_op jit(solution)/shard_map/reduce_max | solution.py:24
  116.5 0.0 all-reduce.3.cloned.1.call-update
  116.6 0.6 stack.2
  117.2 7.3 all-to-all-start.3
  124.5 85.9 %all-reduce.3.cloned.1.call-done = (f32[16,1024]{0,1:T(8,128)}, f32[16,1024]{0,1:T(8,128)}, f32[16,1024]{0,1:T(8,128)}) async-done(((f32[16,1024]{0,1:T(8,128)}, f32[16,1024]{0,1:T(8,128)}, f32[16,1024]{0,1:T(8,128)}), (f32[16,1024]{0,1:T(8,128)}, f32[16,1024]{0,1:T(8,128)}, f32[16,1024]{0,1:T(8,128)})) %all-reduce.3.cloned.1.call-update) | async-done | bytes 196624 | tf_op jit(solution)/shard_map/pmax | solution.py:20
  210.4 23.5 %divide_convert_fusion.1 = (bf16[16,256,1024]{1,0,2:T(8,128)(2,1)}, bf16[16,256,1024]{1,0,2:T(8,128)(2,1)}) fusion(f32[16,256,1024]{1,0,2:T(8,128)} %copy.47, bf16[16,256,1024]{1,0,2:T(8,128)(2,1)} %copy.46, f32[16,1024]{0,1:T(8,128)} %get-tuple-element.15, f32[16,1024]{0,1:T(8,128)} %get-tuple-element.14, f32[16,256,1024]{1,0,2:T(8,128)} %copy.44, ...), kind=kLoop, calls=%fused_computation.3 | loop fusion | flops 33554432 | bytes 67239936 | tf_op jit(solution)/shard_map/convert_element_type | solution.py:30
  233.9 189.3 %all_to_all.59 = bf16[16,256,1024]{1,0,2:T(8,128)(2,1)} all-to-all(bf16[16,256,1024]{1,0,2:T(8,128)(2,1)} %get-tuple-element.18), channel_id=1, replica_groups=mesh['owner'=4,'rows'=8] {'rows'}, dimensions={2} | all-to-all | bytes 16777216 | tf_op jit(solution)/shard_map/all_to_all | solution.py:34
  423.2 4.9 all-to-all-start.1
  428.2 23.8 %divide_convert_fusion = bf16[16,1024,256]{2,0,1:T(8,128)(2,1)} fusion(f32[16,1024,256]{2,1,0:T(8,128)} %param.12, f32[16,1024]{0,1:T(8,128)S(1)} %copy-done.2, bf16[16,1024,256]{2,1,0:T(8,128)(2,1)} %param.13), kind=kLoop, calls=%fused_computation.1 | loop fusion | flops 16777216 | bytes 33619968 | tf_op jit(solution)/shard_map/convert_element_type | solution.py:31
  451.9 158.6 %all-to-all-done.1 = bf16[16,256,1024]{1,0,2:T(8,128)(2,1)} async-done(((bf16[16,256,1024]{1,0,2:T(8,128)(2,1)}), bf16[16,256,1024]{1,0,2:T(8,128)(2,1)}, u32[]{:S(2)}, u32[]{:S(2)}) %all-to-all-start.1) | async-done | bytes 8388640 | tf_op jit(solution)/shard_map/all_to_all | solution.py:35
  610.5 5.0 all-to-all-start.2
  615.6 6.0 all_gather.3
  621.6 0.8 constant_dynamic-slice_fusion
  622.4 0.7 copy.54
  623.1 0.7 copy.55
  623.8 0.8 constant_dynamic-slice_fusion.2
  624.6 0.7 copy.53
  625.3 12.3 %copy.45 = bf16[16,8,256,128]{3,2,1,0:T(8,128)(2,1)} copy(bf16[16,8,256,128]{2,0,3,1:T(8,128)(2,1)} %bitcast.17) | data formatting | bytes 16777216 | tf_op jit(solution)/shard_map/all_to_all | solution.py:34
  637.6 12.3 %copy.48 = bf16[16,8,256,128]{3,2,1,0:T(8,128)(2,1)} copy(bf16[16,8,256,128]{2,0,3,1:T(8,128)(2,1)} %bitcast.4) | data formatting | bytes 16777216 | tf_op jit(solution)/shard_map/all_to_all | solution.py:35
  649.8 147.6 %all-to-all-done.2 = bf16[16,1024,256]{2,0,1:T(8,128)(2,1)} async-done(((bf16[16,1024,256]{2,0,1:T(8,128)(2,1)}), bf16[16,1024,256]{2,0,1:T(8,128)(2,1)}, u32[]{:S(2)}, u32[]{:S(2)}) %all-to-all-start.2) | async-done | bytes 8388640 | tf_op jit(solution)/shard_map/all_to_all | solution.py:37
  797.5 11.4 %copy.51 = bf16[16,128,8,256]{3,2,1,0:T(8,128)(2,1)} copy(bf16[16,128,8,256]{3,0,1,2:T(8,128)(2,1)} %bitcast.7) | data formatting | bytes 16777216 | tf_op jit(solution)/shard_map/all_to_all | solution.py:37
  808.9 13.4 %all_to_all.53 = bf16[16,128,2048]{2,1,0:T(8,128)(2,1)} reshape(bf16[16,128,8,256]{3,2,1,0:T(8,128)(2,1)} %copy.51) | data formatting | bytes 16777216 | tf_op jit(solution)/shard_map/all_to_all | solution.py:37
  822.3 0.7 copy.68
  (16 shorter events, 0.0 us)
Async XLA Ops:
  7.2 203.2 %all-reduce.3.cloned.1.call-start = ((), (), s32[]{:S(2)}) async-start(), calls=%async_computation.4 | async-start | bytes 3145728 | tf_op jit(solution)/shard_map/pmax | solution.py:20
  67.4 13.2 %copy-start = (f32[16,256,1024]{1,0,2:T(8,128)S(1)}, f32[16,256,1024]{1,0,2:T(8,128)}, u32[]{:S(2)}) copy-start(f32[16,256,1024]{1,0,2:T(8,128)} %copy.44) | copy-start | bytes 50331652
  67.4 15.6 %copy-start.1 = (bf16[16,256,1024]{1,0,2:T(8,128)(2,1)S(1)}, bf16[16,256,1024]{1,0,2:T(8,128)(2,1)}, u32[]{:S(2)}) copy-start(bf16[16,256,1024]{1,0,2:T(8,128)(2,1)} %copy.43) | copy-start | bytes 25165828
  67.4 19.9 %slice-start = ((s8[8388608]{0:T(1024)(128)(4,1)}), s8[4194304]{0:T(1024)(128)(4,1)S(1)}, s32[]{:S(2)}) async-start(s8[8388608]{0:T(1024)(128)(4,1)} %bitcast.15), calls=%async_computation.5 | async-start | bytes 8388608
  83.0 4.3 slice-start.1
  87.2 29.3 %copy-start.3 = (f32[256,16]{0,1:T(8,128)S(1)}, f32[256,16]{0,1:T(8,128)}, u32[]{:S(2)}) copy-start(f32[256,16]{0,1:T(8,128)} %param.14) | copy-start | bytes 49156
  87.2 29.3 %copy-start.4 = (f32[256]{0:T(256)S(1)}, f32[256]{0:T(256)}, u32[]{:S(2)}) copy-start(f32[256]{0:T(256)} %param.15) | copy-start | bytes 3076
  117.2 116.7 %all-to-all-start.3 = ((bf16[8,256,16]{1,2,0:T(8,128)(2,1)}), bf16[8,256,16]{1,2,0:T(8,128)(2,1)S(1)}, u32[]{:S(2)}, u32[]{:S(2)}) async-start(bf16[8,256,16]{1,2,0:T(8,128)(2,1)} %stack.2), calls=%async_computation.3 | async-start | bytes 131072 | tf_op jit(solution)/shard_map/all_to_all | solution.py:9
  233.9 194.3 %copy-start.2 = (f32[16,1024]{0,1:T(8,128)S(1)}, f32[16,1024]{0,1:T(8,128)}, u32[]{:S(2)}) copy-start(f32[16,1024]{0,1:T(8,128)} %get-tuple-element.16) | copy-start | bytes 196612
  423.2 187.3 %all-to-all-start.1 = ((bf16[16,256,1024]{1,0,2:T(8,128)(2,1)}), bf16[16,256,1024]{1,0,2:T(8,128)(2,1)}, u32[]{:S(2)}, u32[]{:S(2)}) async-start(bf16[16,256,1024]{1,0,2:T(8,128)(2,1)} %get-tuple-element.17), calls=%async_computation.1 | async-start | bytes 16777216 | tf_op jit(solution)/shard_map/all_to_all | solution.py:35
  610.5 187.0 %all-to-all-start.2 = ((bf16[16,1024,256]{2,0,1:T(8,128)(2,1)}), bf16[16,1024,256]{2,0,1:T(8,128)(2,1)}, u32[]{:S(2)}, u32[]{:S(2)}) async-start(bf16[16,1024,256]{2,0,1:T(8,128)(2,1)} %divide_convert_fusion), calls=%async_computation.2 | async-start | bytes 16777216 | tf_op jit(solution)/shard_map/all_to_all | solution.py:37
Sparse Core Ops, SparseCore 0:
  116.7 93.6 all-reduce.2
